TPU v7x, 128 devices: a whole 4x4x4 slice. The times are simulated.
128 devices in a mesh: rows: 32 (over z, y, core), cols: 4 (over x).
Axes of the slice: x: 4, y: 4, z: 4, core: 2. Of those that a mesh axis runs over, the one named last changes fastest.
Arguments:
- w_gate: float32 [2048, 8192], P('rows', 'cols'), may hold values from -0.25 to 0.25
- first_gate: float32 [2048, 8192], P('rows', 'cols'), may hold values from -6 to 6
- second_gate: float32 [2048, 8192], P('rows', 'cols'), may hold values from 0.1 to 10
- w_up: float32 [2048, 8192], P('rows', 'cols'), may hold values from -0.25 to 0.25
- first_up: float32 [2048, 8192], P('rows', 'cols'), may hold values from -6 to 6
- second_up: float32 [2048, 8192], P('rows', 'cols'), may hold values from 0.1 to 10
- norm_train: float32 [2048], P(('rows', 'cols')), may hold values from 0.25 to 1.75
- norm_step: float32 [2048], P(('rows', 'cols')), may hold values from -0.3 to 0.3
Outputs:
- ready_gate: bfloat16 [2048, 8192], P(None, 'cols')
- ready_up: bfloat16 [2048, 8192], P(None, 'cols')
- column_gate: float32 [8192], P('cols')
- column_up: float32 [8192], P('cols')
- serve_norm: bfloat16 [2048], replicated
- latest_gate: float32 [2048, 8192], P('rows', 'cols')
- latest_up: float32 [2048, 8192], P('rows', 'cols')
All inputs are finite; a program needn't handle non-finite values. Where the computation divides by a largest or mean magnitude, that divisor is 1e-20 or more.
Results may differ from a plain program's by a relative error of at most 0.001.
Values may be sent and summed in bfloat16 or wider, within the bound.
No kernel may reach another device: no remote copies, remote signals or barrier semaphores. Data moves between devices by JAX's collectives and lax.ppermute only.
A program may use at most 128 MiB of HBM per device.

v0:
```python
import jax
import jax.numpy as jnp
from jax import lax
from jax.sharding import Mesh
from jax.sharding import PartitionSpec as P

D_MODEL = 2048
ROWS = ("rows_0", "rows_1", "rows_2")
ROWS_COLS = ("rows_0", "rows_1", "rows_2", "cols")


learn_rate = 0.01
decay_rate = 0.1
tiny_value = 1e-08


def from_everyone(value, axis):
    length = lax.axis_size(axis)
    return lax.all_to_all(
        jnp.broadcast_to(value[None], (length, *value.shape)), axis, 0, 0, tiled=True
    )


def of_everyone(value, axis):
    return from_everyone(value, axis).sum(axis=0)


def together(arrays, axis):
    ends = [0]
    for a in arrays:
        ends.append(ends[-1] + a.size)
    so_far = of_everyone(jnp.concatenate([a.ravel() for a in arrays]), axis)
    return tuple((so_far[b:e].reshape(a.shape) for a, b, e in zip(arrays, ends, ends[1:])))


def sent_together(arrays, axis, dim, along):
    ends, at = ([], 0)
    for a in arrays[:-1]:
        at += a.shape[along]
        ends.append(at)
    both = jnp.concatenate(arrays, axis=along)
    return tuple(jnp.split(lax.all_gather(both, axis, axis=dim, tiled=True), ends, axis=along))


def joined_along(pieces, dim):
    lengths = list(pieces.shape[1:])
    lengths[dim] *= pieces.shape[0]
    return jnp.moveaxis(pieces, 0, dim).reshape(lengths)


def stacked_from(value, axes, order):
    pieces = value[None]
    for k in order:
        pieces = lax.all_gather(pieces, axes[k], axis=0, tiled=True)
    current = [lax.axis_size(axes[k]) for k in reversed(order)]
    pieces = pieces.reshape(*current, *value.shape)
    turned = sorted(range(len(order)), key=lambda place: order[len(order) - 1 - place])
    return pieces.transpose(*turned, *range(len(order), pieces.ndim)).reshape(-1, *value.shape)


def gather_axes(value, axes, order, dim):
    return joined_along(stacked_from(value, axes, order), dim)


def local(w_gate, first_gate, second_gate, w_up, first_up, second_up, norm_train, norm_step):
    latest_gate = w_gate - learn_rate * (
        first_gate / (jnp.sqrt(second_gate) + tiny_value) + decay_rate * w_gate
    )
    latest_up = w_up - learn_rate * (
        first_up / (jnp.sqrt(second_up) + tiny_value) + decay_rate * w_up
    )
    total_gate, total_up = together(
        (jnp.sum(jnp.abs(latest_gate), axis=0), jnp.sum(jnp.abs(latest_up), axis=0)), ROWS
    )
    column_gate = total_gate / D_MODEL
    column_up = total_up / D_MODEL
    narrow_gate, narrow_up = (
        (latest_gate / column_gate).astype(jnp.bfloat16),
        (latest_up / column_up).astype(jnp.bfloat16),
    )
    ready_gate, ready_up = sent_together((narrow_gate, narrow_up), ROWS, 0, 1)
    serve_norm = gather_axes(
        (norm_train + norm_step).astype(jnp.bfloat16), ROWS_COLS, (0, 1, 3, 2), 0
    )
    return (ready_gate, ready_up, column_gate, column_up, serve_norm, latest_gate, latest_up)


def solution(mesh):
    torus = Mesh(
        mesh.devices.reshape(4, 4, 2, mesh.shape["cols"]), ("rows_0", "rows_1", "rows_2", "cols")
    )
    in_specs = (
        P(ROWS, "cols"),
        P(ROWS, "cols"),
        P(ROWS, "cols"),
        P(ROWS, "cols"),
        P(ROWS, "cols"),
        P(ROWS, "cols"),
        P(ROWS_COLS),
        P(ROWS_COLS),
    )
    out_specs = (
        P(None, "cols"),
        P(None, "cols"),
        P("cols"),
        P("cols"),
        P(),
        P(ROWS, "cols"),
        P(ROWS, "cols"),
    )
    return jax.shard_map(local, mesh=torus, in_specs=in_specs, out_specs=out_specs, check_vma=False)
```

profile of v0, /device:TPU:1, one launch (start us, length us, event | category | flops | bytes accessed | tf_op | source)
XLA Modules:
  0.0 121.9 jit_solution(6254912166650149929)
XLA Ops:
  7.2 0.0 copy-start.6
  7.2 0.0 all-gather.5.cloned.1.call-start
  7.2 2.4 %abs_reduce_fusion = (f32[2048]{0:T(1024)S(1)}, f32[64,2048]{1,0:T(8,128)S(1)}, f32[2048]{0:T(1024)S(1)}, f32[64,2048]{1,0:T(8,128)S(1)}) fusion(f32[64,2048]{1,0:T(8,128)} %param.11, f32[64,2048]{1,0:T(8,128)} %param.12, f32[64,2048]{1,0:T(8,128)} %param.13, f32[64,2048]{1,0:T(8,128)} %param.8, f32[64,2048]{1,0:T(8,128)} %param.9, f32[64,2048]{1,0:T(8,128)} %param.10), kind=kLoop, calls=%fused_computation.3 | loop fusion | flops 2093056 | bytes 4210688 | tf_op jit(solution)/shard_map/reduce_sum | solution.py:73
  9.7 0.0 copy-start
  9.7 0.0 copy-start.1
  9.7 0.5 broadcast_in_dim.4
  10.2 20.8 %all_to_all.6 = f32[32,1,4096]{2,1,0:T(1,128)S(1)} all-to-all(f32[32,1,4096]{2,1,0:T(1,128)S(1)} %broadcast_in_dim.4), channel_id=1, replica_groups=mesh['rows_0'=4,'rows_1'=4,'rows_2'=2,'cols'=4] {'rows_0','rows_1','rows..., dimensions={0} | all-to-all | bytes 1048576 | tf_op jit(solution)/shard_map/all_to_all | solution.py:19
  31.0 0.4 reduce_sum.29
  31.4 0.0 copy-start.2
  31.4 0.0 copy-start.3
  31.5 0.8 pad_maximum_fusion
  32.3 0.0 all-gather.5.cloned.1.call-update
  32.4 0.6 dynamic-slice
  33.6 0.2 dynamic-update-slice
  33.9 6.8 %all-reduce = bf16[64]{0:T(256)(128)(2,1)S(1)} all-reduce(bf16[64]{0:T(256)(128)(2,1)S(1)} %dynamic-update-slice), channel_id=2, replica_groups=mesh['rows_0'=4,'rows_1'=4,'rows_2'=2,'cols'=4] {'rows_0'}, use_global_device_ids=true, to_apply=%add | all-reduce | flops 64 | bytes 256
  40.7 0.1 reshape.30
  40.8 7.7 %all-gather.1 = bf16[4,4,16]{2,1,0:T(4,128)(2,1)S(1)} all-gather(bf16[1,4,16]{2,1,0:T(4,128)(2,1)S(1)} %reshape.30), channel_id=1, replica_groups=mesh['rows_0'=4,'rows_1'=4,'rows_2'=2,'cols'=4] {'rows_1'}, dimensions={0}, use_global_device_ids=true | all-gather | bytes 640 | tf_op jit(solution)/shard_map/all_gather | solution.py:54
  48.5 9.8 %all_gather.18 = bf16[64,16]{1,0:T(8,128)(2,1)S(1)} all-gather(bf16[16,16]{1,0:T(8,128)(2,1)S(1)} %bitcast.8), channel_id=1, replica_groups=mesh['rows_0'=4,'rows_1'=4,'rows_2'=2,'cols'=4] {'cols'}, dimensions={0}, use_global_device_ids=true | all-gather | bytes 2560 | tf_op jit(solution)/shard_map/all_gather | solution.py:54
  58.4 0.1 copy.26
  58.5 6.4 %all-gather.2 = bf16[2,64,16]{1,2,0:T(8,128)(2,1)S(1)} all-gather(bf16[1,64,16]{1,2,0:T(8,128)(2,1)S(1)} %copy.26), channel_id=1, replica_groups=mesh['rows_0'=4,'rows_1'=4,'rows_2'=2,'cols'=4] {'rows_2'}, dimensions={0}, use_global_device_ids=true | all-gather | bytes 6144 | tf_op jit(solution)/shard_map/all_gather | solution.py:54
  64.9 0.1 copy.27
  65.0 0.7 reshape_reshape.3
  65.7 37.4 %all-gather.5.cloned.1.call-done = bf16[2048,4096]{1,0:T(8,128)(2,1)} async-done(((bf16[64,4096]{1,0:T(8,128)(2,1)}), bf16[2048,4096]{1,0:T(8,128)(2,1)}) %all-gather.5.cloned.1.call-update) | async-done | bytes 16777232 | tf_op jit(solution)/shard_map/all_gather | solution.py:42
  103.1 11.9 %fusion = (bf16[2048,2048]{1,0:T(8,128)(2,1)}, bf16[2048,2048]{1,0:T(8,128)(2,1)}) fusion(bf16[2048,4096]{1,0:T(8,128)(2,1)} %all-gather.5.cloned.1.call-done), kind=kLoop, calls=%fused_computation.11 | loop fusion | bytes 33554432 | tf_op jit(solution)/shard_map/split | solution.py:42
  (16 shorter events, 0.1 us)
Async XLA Ops:
  7.2 25.2 %copy-start.6 = (u32[128]{0:T(128)S(1)}, u32[128]{0:T(128)}, u32[]{:S(2)}) copy-start(u32[128]{0:T(128)} %constant.16) | copy-start | bytes 1540
  7.2 26.4 %copy-start.4 = (f32[16]{0:T(128)S(1)}, f32[16]{0:T(128)}, u32[]{:S(2)}) copy-start(f32[16]{0:T(128)} %param.14) | copy-start | bytes 196
  7.2 26.4 %copy-start.5 = (f32[16]{0:T(128)S(1)}, f32[16]{0:T(128)}, u32[]{:S(2)}) copy-start(f32[16]{0:T(128)} %param.15) | copy-start | bytes 196
  7.2 95.9 %all-gather.5.cloned.1.call-start = ((), (), s32[]{:S(2)}) async-start(), calls=%async_computation.1 | async-start | bytes 17301504 | tf_op jit(solution)/shard_map/all_gather | solution.py:42
  9.7 105.4 %copy-start = (f32[64,2048]{1,0:T(8,128)}, f32[64,2048]{1,0:T(8,128)S(1)}, u32[]{:S(2)}) copy-start(f32[64,2048]{1,0:T(8,128)S(1)} %get-tuple-element.10) | copy-start | bytes 1572868
  9.7 105.4 %copy-start.1 = (f32[64,2048]{1,0:T(8,128)}, f32[64,2048]{1,0:T(8,128)S(1)}, u32[]{:S(2)}) copy-start(f32[64,2048]{1,0:T(8,128)S(1)} %get-tuple-element.16) | copy-start | bytes 1572868
  31.4 83.7 %copy-start.2 = (f32[2048]{0:T(1024)}, f32[2048]{0:T(1024)S(1)}, u32[]{:S(2)}) copy-start(f32[2048]{0:T(1024)S(1)} %get-tuple-element.13) | copy-start | bytes 24580
  31.4 83.7 %copy-start.3 = (f32[2048]{0:T(1024)}, f32[2048]{0:T(1024)S(1)}, u32[]{:S(2)}) copy-start(f32[2048]{0:T(1024)S(1)} %get-tuple-element.14) | copy-start | bytes 24580
Sparse Core Ops, SparseCore 0:
  32.5 70.5 all-gather.4
where the time goes:
time: 122 us
  blocking collectives  51.6 us (42%)
  waiting for transfers between devices  37.4 us (31%)
  between operations  14.9 us (12%)
  local copies, waits for them, and re-layouts  14.3 us (12%)
  other arithmetic  3.7 us (3%)
    all_gather x1, waiting for transfers between devices, sent_together(): lax.all_gather(both, axis, axis=dim, tiled=True)  37.4 us
    all_gather x3, blocking collectives, stacked_from(): pieces = lax.all_gather(pieces, axes[k], axis=0, tiled=True)  24 us
    all_to_all x1, blocking collectives, from_everyone(): lax.all_to_all(jnp.broadcast_to(value[None], (length, *value.shape)), axi...  20.8 us
    split x1, local copies, waits for them, and re-layouts, sent_together(): jnp.split(lax.all_gather(both, axis, axis=dim, tiled=True), ends, axis=al...  11.9 us
    unnamed x1, blocking collectives  6.83 us
  transfers between devices with their start and end apart: 1, of which 1 were waited for; matrix products, arithmetic and copies ran while one was open for 1% of the time, Pallas kernels for 0%

commit v1 on v0

v1 whole, which is shorter than its diff:
```python
import functools
import jax
import jax.numpy as jnp
from jax import lax
from jax.experimental import pallas as pl
from jax.experimental.pallas import tpu as pltpu
from jax.sharding import Mesh
from jax.sharding import PartitionSpec as P

D_MODEL = 2048
ROWS = ("z", "y", "core")
ALL = ("z", "y", "core", "x")

learn_rate = 0.01
decay_rate = 0.1
tiny_value = 1e-08

OCTAVES = 252.0
LOWEST = -125.0
SLABS = 16
BLOCK = 64 * SLABS + SLABS
VMEM = pl.BlockSpec(memory_space=pltpu.VMEM)
HBM = pl.BlockSpec(memory_space=pltpu.HBM)
SMALL = pltpu.CompilerParams(vmem_limit_bytes=4 << 20)


def number(z, y, c):
    return (z % 4 * 4 + y % 4) * 2 + c


def near_far(by_near, by_far):
    return [
        (number(z, y, c), number(z + by_far, y + by_near, c) if c == 0 else number(z + by_near, y + by_far, c))
        for z in range(4)
        for y in range(4)
        for c in range(2)
    ]


def near(value, by):
    return lax.ppermute(value, ROWS, near_far(by, 0))


def far(value, by):
    return lax.ppermute(value, ROWS, near_far(0, by))


def swapped(value):
    return lax.ppermute(value, "core", [(0, 1), (1, 0)])


def step_kernel(w_g, f_g, s_g, w_u, f_u, s_u, latest_g, latest_u, code, sums, *scratch):
    held, sem = scratch[:6], scratch[6]
    wide = 512
    chunks = D_MODEL // wide
    sources = (w_g, f_g, s_g, w_u, f_u, s_u)
    copies = []
    for k in range(chunks):
        at = pl.ds(k * wide, wide)
        for i in range(6):
            one = pltpu.make_async_copy(sources[i].at[:, at], held[i].at[:, at], sem.at[k * 6 + i])
            one.start()
            copies.append(one)
    for k in range(chunks):
        for o, latest in ((0, latest_g), (1, latest_u)):
            for i in range(3):
                copies[k * 6 + 3 * o + i].wait()
            for slab in range(k * wide // 128, (k + 1) * wide // 128):
                at = pl.ds(slab * 128, 128)
                w, first, second = (held[3 * o + i][:, at] for i in range(3))
                new = w - learn_rate * (first / (jnp.sqrt(second) + tiny_value) + decay_rate * w)
                latest[:, at] = new
                size = jnp.abs(new)
                sums[pl.ds(SLABS * o + slab, 1), :] = jnp.sum(size, axis=0, keepdims=True)
                top = (jnp.max(size, axis=0, keepdims=True) * 1.01).astype(jnp.bfloat16)
                scale = OCTAVES / jnp.maximum(top.astype(jnp.float32), 1e-35)
                value = jnp.exp2(size * scale + LOWEST)
                code[pl.ds(BLOCK * o + 64 * slab, 64), :] = jnp.where(new < 0, -value, value).astype(jnp.bfloat16)
                scratch[7][pl.ds(SLABS * o + slab, 1), :] = top.astype(jnp.float32)
    for o in (0, 1):
        code[pl.ds(BLOCK * o + 64 * SLABS, SLABS), :] = scratch[7][pl.ds(SLABS * o, SLABS), :].astype(jnp.bfloat16)


def stepped(*arrays):
    weights = jax.ShapeDtypeStruct((64, D_MODEL), jnp.float32)
    return pl.pallas_call(
        step_kernel,
        out_shape=(
            weights,
            weights,
            jax.ShapeDtypeStruct((2 * BLOCK, 128), jnp.bfloat16),
            jax.ShapeDtypeStruct((2 * SLABS, 128), jnp.float32),
        ),
        in_specs=[HBM] * 6,
        out_specs=(VMEM,) * 4,
        scratch_shapes=[pltpu.VMEM((64, D_MODEL), jnp.float32)] * 6
        + [pltpu.SemaphoreType.DMA((24,)), pltpu.VMEM((2 * SLABS, 128), jnp.float32)],
        compiler_params=pltpu.CompilerParams(vmem_limit_bytes=8 << 20),
        name="step",
    )(*arrays)


def pack_kernel(spans, *refs):
    out, at = refs[-1], 0
    for ref, (lo, n) in zip(refs, spans):
        for k in range(0, n, 208):
            out[pl.ds(at + k, 208), :] = ref[pl.ds(lo + k, 208), :]
        at += n


def packed(*parts):
    spans = tuple((lo * BLOCK, n * BLOCK) for _, lo, n in parts)
    return pl.pallas_call(
        functools.partial(pack_kernel, spans),
        out_shape=jax.ShapeDtypeStruct((sum(n for _, n in spans), 128), jnp.bfloat16),
        in_specs=[VMEM] * len(parts),
        out_specs=VMEM,
        compiler_params=SMALL,
        name="pack",
    )(*(a for a, _, _ in parts))


def home(core_away, a, b):
    z, y, c = (lax.axis_index(axis) for axis in ROWS)
    c = lax.rem(c + core_away, 2)
    dz, dy = a + (b - a) * (1 - c), b + (a - b) * (1 - c)
    at = (lax.rem(z + 4 - dz, 4) * 4 + lax.rem(y + 4 - dy, 4)) * 2 + c
    return pl.ds(pl.multiple_of(at * 64, 64), 64)


def decode_kernel(plan, write, n, *refs):
    arrays, total = refs[:n], refs[n]
    plain, factor = (refs[-5], refs[-1]) if write else (refs[-2], refs[-1])
    outs, sem = (refs[-4:-2], refs[-2]) if write else (None, None)
    copies = []
    for k, (i, at, o, a, b) in enumerate(plan):
        ref = arrays[i]
        inverse = (D_MODEL / OCTAVES) / total[pl.ds(SLABS * o, SLABS), :]
        factor[...] = ref[pl.ds(at * BLOCK + 64 * SLABS, SLABS), :].astype(jnp.float32) * inverse

        def slab(j, carry, ref=ref, at=at, k=k):
            rows = pl.ds(pl.multiple_of(at * BLOCK + j * 64, 16), 64)
            value = ref[rows, :].astype(jnp.float32)
            size = (jnp.log2(jnp.abs(value)) - LOWEST) * factor[pl.ds(j, 1), :]
            plain[pl.ds(64 * k, 64), pl.ds(pl.multiple_of(j * 128, 128), 128)] = jnp.where(
                value < 0, -size, size
            ).astype(jnp.bfloat16)
            return carry

        lax.fori_loop(0, SLABS, slab, 0, unroll=2)
        if write:
            one = pltpu.make_async_copy(plain.at[pl.ds(64 * k, 64), :], outs[o].at[home(0, a, b), :], sem.at[k])
            one.start()
            copies.append(one)
    for one in copies:
        one.wait()


READY = jax.ShapeDtypeStruct((D_MODEL, D_MODEL), jnp.bfloat16)


def decoded(outs, arrays, plan, total, write=True):
    n, fresh = len(arrays), outs is None
    plain = jax.ShapeDtypeStruct((64 * len(plan), D_MODEL), jnp.bfloat16)
    got = pl.pallas_call(
        functools.partial(decode_kernel, plan, write, n),
        out_shape=(plain, READY, READY) if write else plain,
        in_specs=[VMEM] * (n + 1) + ([HBM] * 2 if write and not fresh else []),
        out_specs=(VMEM, HBM, HBM) if write else VMEM,
        scratch_shapes=([pltpu.SemaphoreType.DMA((len(plan),))] if write else [])
        + [pltpu.VMEM((SLABS, 128), jnp.float32)],
        input_output_aliases={n + 1: 1, n + 2: 2} if write and not fresh else {},
        compiler_params=SMALL,
    )(*arrays, total, *(outs if write and not fresh else ()))
    return (got[0], got[1:]) if write else (got, outs)


def write_kernel(plan, *refs):
    n = len(plan)
    arrays, outs, sem = refs[:n], refs[-3:-1], refs[-1]
    copies = []
    for ref, (core_away, blocks) in zip(arrays, plan):
        for k, (o, a, b) in enumerate(blocks):
            copies.append(
                pltpu.make_async_copy(
                    ref.at[pl.ds(64 * k, 64), :], outs[o].at[home(core_away, a, b), :], sem.at[len(copies)]
                )
            )
    for one in copies:
        one.start()
    for one in copies:
        one.wait()


def written(outs, batch):
    n = len(batch)
    plan = tuple((core_away, tuple(p[2:] for p in blocks)) for _, core_away, blocks in batch)
    return pl.pallas_call(
        functools.partial(write_kernel, plan),
        out_shape=(READY, READY),
        in_specs=[VMEM] * n + [HBM] * 2,
        out_specs=(HBM, HBM),
        scratch_shapes=[pltpu.SemaphoreType.DMA((sum(len(b) for _, b in plan),))],
        input_output_aliases={n: 0, n + 1: 1},
        compiler_params=SMALL,
    )(*(a for a, _, _ in batch), *outs)


def local(w_gate, first_gate, second_gate, w_up, first_up, second_up, norm_train, norm_step):
    latest_gate, latest_up, own, sums = stepped(w_gate, first_gate, second_gate, w_up, first_up, second_up)
    r, l = near(own, 1), near(own, 3)

    me = (lax.axis_index("z") * 4 + lax.axis_index("y")) * 2 + lax.axis_index("core")
    gain = (norm_train + norm_step).astype(jnp.bfloat16).astype(jnp.float32)
    spread = lax.dynamic_update_slice(
        jnp.zeros((128, 16), jnp.float32), gain[None], (me * 4 + lax.axis_index("x"), 0)
    )
    sums = jnp.concatenate((sums, spread.reshape(SLABS, 128)), axis=0)
    sums = sums + far(sums, 1) + far(sums, 3) + far(sums, 2)
    sums = sums + near(sums, 1) + near(sums, 3) + near(sums, 2)
    sums = sums + swapped(sums)
    column_gate = sums[:SLABS].reshape(D_MODEL) / D_MODEL
    column_up = sums[SLABS : 2 * SLABS].reshape(D_MODEL) / D_MODEL
    norm = sums[2 * SLABS :]
    for by in (1, 3, 2):
        other = lax.ppermute(sums[2 * SLABS :], "x", [(i, (i + by) % 4) for i in range(4)])
        norm = norm + other
    serve_norm = norm.reshape(D_MODEL).astype(jnp.bfloat16)
    total = sums[: 2 * SLABS]

    fa = {by: far(own, by) for by in (1, 3)}
    og, ou = near(packed((r, 0, 1)), 1), near(packed((l, 1, 1)), 3)
    rl = packed((r, 0, 1), (l, 0, 1), (r, 1, 1), (l, 1, 1))
    fb = {by: far(rl, by) for by in (1, 3)}
    o = packed((og, 0, 1), (ou, 0, 1))
    fc = {by: far(o, by) for by in (1, 3)}
    ga_g = far(packed((fa[1], 0, 1), (fb[1], 0, 2)), 1)
    ga_u = far(packed((fa[3], 1, 1), (fb[3], 2, 2)), 3)
    gb_g = far(packed((fc[1], 0, 1)), 1)
    gb_u = far(packed((fc[3], 1, 1)), 3)

    def pair(i, a, b):
        return [(i, 0, 0, a, b), (i, 1, 1, a, b)]

    def four(i, b):
        return [(i, 0, 0, 1, b), (i, 1, 0, 3, b), (i, 2, 1, 1, b), (i, 3, 1, 3, b)]

    batches = [
        ([own, rl, o, fa[1], fa[3]], pair(0, 0, 0) + four(1, 0) + pair(2, 2, 0) + pair(3, 0, 1) + pair(4, 0, 3)),
        ([fb[1], fb[3]], four(0, 1) + four(1, 3)),
        ([fc[1], fc[3]], pair(0, 2, 1) + pair(1, 2, 3)),
        ([ga_g, ga_u], [(o, i, o, a, 2) for o in (0, 1) for i, a in enumerate((0, 1, 3))]),
        ([gb_g, gb_u], [(o, 0, o, 2, 2) for o in (0, 1)]),
    ]
    outs = None
    for j, (arrays, plan) in enumerate(batches):
        last = j == len(batches) - 1
        plain, outs = decoded(outs, arrays, tuple(plan), total, write=not last)
        other = swapped(plain)
        outs = written(outs, ([(plain, 0, plan)] if last else []) + [(other, 1, plan)])
    return (outs[0], outs[1], column_gate, column_up, serve_norm, latest_gate, latest_up)


def solution(mesh):
    torus = Mesh(mesh.devices.reshape(4, 4, 2, mesh.shape["cols"]), ALL)
    whole = P(ROWS, "x")
    return jax.shard_map(
        local,
        mesh=torus,
        in_specs=(whole,) * 6 + (P(ALL),) * 2,
        out_specs=(P(None, "x"), P(None, "x"), P("x"), P("x"), P(), whole, whole),
        check_vma=False,
    )
```

time: 122 us -> 109 us (0.89)
  blocking collectives: 51.6 us -> 0 us
  starting transfers between devices: 0.04 us -> 44 us
  Pallas kernels: 0 us -> 19.6 us
  between operations: 14.9 us -> 0.84 us
  local copies, waits for them, and re-layouts: 14.3 us -> 6.37 us
  other arithmetic: 3.7 us -> 1.3 us
  waiting for transfers between devices: 37.4 us -> 36.1 us
    ppermute x0 -> x29, starting transfers between devices: none -> 44 us  [the longest x13 19.4 us: far(): return lax.ppermute(value, ROWS, near_far(0, by))]
    all_gather x1 -> x0, waiting for transfers between devices: 37.4 us -> none  [sent_together(): lax.all_gather(both, axis, axis=dim, tiled=True)]
    ppermute x0 -> x29, waiting for transfers between devices: none -> 36.1 us  [the longest x13 27 us: far(): return lax.ppermute(value, ROWS, near_far(0, by))]
    all_gather x3 -> x0, blocking collectives: 24 us -> none  [stacked_from(): pieces = lax.all_gather(pieces, axes[k], axis=0, tiled=True)]
    all_to_all x1 -> x0, blocking collectives: 20.8 us -> none  [from_everyone(): lax.all_to_all(jnp.broadcast_to(value[None], (length, *value.shape)), axi...]
    pallas_call x0 -> x19, Pallas kernels: none -> 19.6 us  [the longest x5 10.3 us: decoded(): pl.pallas_call(functools.partial(decode_kernel, plan, write, n), out_shap...]
    split x1 -> x0, local copies, waits for them, and re-layouts: 11.9 us -> none  [sent_together(): jnp.split(lax.all_gather(both, axis, axis=dim, tiled=True), ends, axis=al...]
    unnamed x1 -> x0, blocking collectives: 6.83 us -> none
  transfers between devices with their start and end apart: 1 -> 29, of which waited for: 1 -> 12; matrix products, arithmetic and copies ran while one was open for 1% -> 1% of each run, Pallas kernels for 0% -> 6%
where the time goes in v1:
time: 109 us; the launch traced here: 108 us
  starting transfers between devices  44 us (40%)
  waiting for transfers between devices  36.1 us (33%)
  Pallas kernels  19.6 us (18%)
  local copies, waits for them, and re-layouts  6.37 us (6%)
  other arithmetic  1.3 us (1%)
    ppermute x13, waiting for transfers between devices, far(): return lax.ppermute(value, ROWS, near_far(0, by))  27 us
    ppermute x13, starting transfers between devices, far(): return lax.ppermute(value, ROWS, near_far(0, by))  19.4 us
    pallas_call x5, Pallas kernels, decoded(): pl.pallas_call(functools.partial(decode_kernel, plan, write, n), out_shap...  10.3 us
    ppermute x6, starting transfers between devices, swapped(): return lax.ppermute(value, 'core', [(0, 1), (1, 0)])  10.2 us
    ppermute x7, starting transfers between devices, near(): return lax.ppermute(value, ROWS, near_far(by, 0))  10.2 us
    pallas_call x5, Pallas kernels, written(): pl.pallas_call(functools.partial(write_kernel, plan), out_shape=(READY, R...  6.32 us
    unnamed x13, local copies, waits for them, and re-layouts  6.24 us
    ppermute x3, starting transfers between devices, local(): lax.ppermute(sums[2 * SLABS:], 'x', [(i, (i + by) % 4) for i in range(4)])  4.21 us
  transfers between devices with their start and end apart: 29, of which 12 were waited for; matrix products, arithmetic and copies ran while one was open for 1% of the time, Pallas kernels for 6%

profile of v1, /device:TPU:1, one launch (start us, length us, event | category | flops | bytes accessed | tf_op | source)
XLA Modules:
  0.0 108.3 jit_solution(5346347530490465633)
XLA Ops:
  6.9 2.7 %step.1 = (f32[64,2048]{1,0:T(8,128)}, f32[64,2048]{1,0:T(8,128)}, bf16[2080,128]{1,0:T(8,128)(2,1)S(1)}, f32[32,128]{1,0:T(8,128)S(1)}) custom-call(f32[64,2048]{1,0:T(8,128)S(1)} %copy-done, f32[64,2048]{1,0:T(8,128)S(1)} %copy-done.1, f32[64,2048]{1,0:T(8,128)S(1)} %copy-done.2, f32[64,2048]{1,0:T(8,128)S(1)} %copy-done.3, f32[64,2048]{1,0:T(8,128)S(1)} %copy-done.4, ...), custom_call_target="tpu_custom_call" | custom-call | tf_op jit(solution)/shard_map/step/pallas_call | solution.py:86
  9.6 2.5 %collective-permute-start = (bf16[2080,128]{1,0:T(8,128)(2,1)S(1)}, bf16[2080,128]{1,0:T(8,128)(2,1)S(1)}, u32[]{:S(2)}, u32[]{:S(2)}) collective-permute-start(bf16[2080,128]{1,0:T(8,128)(2,1)S(1)} %get-tuple-element.33.refs_0_), channel_id=1, source_target_pairs={{0,8},{4,36},{8,16},{12,44},{16,24},{20,52},{24,0},{28,60},{32,40}... | collective-permute-start | bytes 1597448 | tf_op jit(solution)/shard_map/ppermute | solution.py:41
  12.2 2.2 %collective-permute-start.2 = (bf16[2080,128]{1,0:T(8,128)(2,1)S(1)}, bf16[2080,128]{1,0:T(8,128)(2,1)S(1)}, u32[]{:S(2)}, u32[]{:S(2)}) collective-permute-start(bf16[2080,128]{1,0:T(8,128)(2,1)S(1)} %get-tuple-element.33.refs_0_), channel_id=1, source_target_pairs={{0,24},{4,100},{8,0},{12,108},{16,8},{20,116},{24,16},{28,124},{32... | collective-permute-start | bytes 1597448 | tf_op jit(solution)/shard_map/ppermute | solution.py:41
  15.2 3.0 %collective-permute-start.10 = (f32[48,128]{1,0:T(8,128)S(1)}, f32[48,128]{1,0:T(8,128)S(1)}, u32[]{:S(2)}, u32[]{:S(2)}) collective-permute-start(f32[48,128]{1,0:T(8,128)S(1)} %constant_dynamic-update-slice_fusion), channel_id=1, source_target_pairs={{0,64},{4,20},{8,72},{12,28},{16,80},{20,4},{24,88},{28,12},{32,96... | collective-permute-start | bytes 73736 | tf_op jit(solution)/shard_map/ppermute | solution.py:45
  18.6 2.3 %collective-permute-start.9 = (f32[48,128]{1,0:T(8,128)S(1)}, f32[48,128]{1,0:T(8,128)S(1)}, u32[]{:S(2)}, u32[]{:S(2)}) collective-permute-start(f32[48,128]{1,0:T(8,128)S(1)} %constant_dynamic-update-slice_fusion), channel_id=1, source_target_pairs={{0,96},{4,28},{8,104},{12,4},{16,112},{20,12},{24,120},{28,20},{32... | collective-permute-start | bytes 73736 | tf_op jit(solution)/shard_map/ppermute | solution.py:45
  23.6 2.7 %collective-permute-start.12 = (f32[48,128]{1,0:T(8,128)S(1)}, f32[48,128]{1,0:T(8,128)S(1)}, u32[]{:S(2)}, u32[]{:S(2)}) collective-permute-start(f32[48,128]{1,0:T(8,128)S(1)} %add_add_fusion.1), channel_id=1, source_target_pairs={{0,24},{4,100},{8,0},{12,108},{16,8},{20,116},{24,16},{28,124},{32... | collective-permute-start | bytes 73736 | tf_op jit(solution)/shard_map/ppermute | solution.py:41
  26.4 1.7 %collective-permute-done.11 = f32[48,128]{1,0:T(8,128)S(1)} collective-permute-done((f32[48,128]{1,0:T(8,128)S(1)}, f32[48,128]{1,0:T(8,128)S(1)}, u32[]{:S(2)}, u32[]{:S(2)}) %collective-permute-start.11) | collective-permute-done | bytes 24608 | tf_op jit(solution)/shard_map/ppermute | solution.py:41
  28.1 2.7 %collective-permute-start.3 = (bf16[1040,128]{1,0:T(8,128)(2,1)S(1)}, bf16[1040,128]{1,0:T(8,128)(2,1)S(1)}, u32[]{:S(2)}, u32[]{:S(2)}) collective-permute-start(bf16[1040,128]{1,0:T(8,128)(2,1)S(1)} %pack.9), channel_id=1, source_target_pairs={{0,24},{4,100},{8,0},{12,108},{16,8},{20,116},{24,16},{28,124},{32... | collective-permute-start | bytes 798728 | tf_op jit(solution)/shard_map/ppermute | solution.py:41
  30.8 3.6 %collective-permute-start.14 = (f32[48,128]{1,0:T(8,128)S(1)}, f32[48,128]{1,0:T(8,128)S(1)}, u32[]{:S(2)}, u32[]{:S(2)}) collective-permute-start(f32[48,128]{1,0:T(8,128)S(1)} %add_add_fusion), channel_id=1, source_target_pairs={{0,4},{4,0},{1,5},{5,1},{2,6},{6,2},{3,7},{7,3},{8,12},{12,8},{9,1... | collective-permute-start | bytes 73736 | tf_op jit(solution)/shard_map/ppermute | solution.py:49
  36.3 3.5 %shard_map.136 = (bf16[768,2048]{1,0:T(8,128)(2,1)S(1)}, bf16[2048,2048]{1,0:T(8,128)(2,1)}, bf16[2048,2048]{1,0:T(8,128)(2,1)}) custom-call(bf16[2080,128]{1,0:T(8,128)(2,1)S(1)} %get-tuple-element.33.refs_0_, bf16[4160,128]{1,0:T(8,128)(2,1)S(1)} %pack.13.refs_1_, bf16[2080,128]{1,0:T(8,128)(2,1)S(1)} %pack.10.refs_2_, ...), custom_call_target="tpu_custom_call" | custom-call | tf_op jit(solution)/shard_map/pallas_call | solution.py:165
  39.8 2.5 %collective-permute-start.22 = (bf16[768,2048]{1,0:T(8,128)(2,1)S(1)}, bf16[768,2048]{1,0:T(8,128)(2,1)S(1)}, u32[]{:S(2)}, u32[]{:S(2)}) collective-permute-start(bf16[768,2048]{1,0:T(8,128)(2,1)S(1)} %get-tuple-element.35), channel_id=1, source_target_pairs={{0,4},{4,0},{1,5},{5,1},{2,6},{6,2},{3,7},{7,3},{8,12},{12,8},{9,1... | collective-permute-start | bytes 9437192 | tf_op jit(solution)/shard_map/ppermute | solution.py:49
  42.4 2.9 %collective-permute-start.20 = (bf16[4160,128]{1,0:T(8,128)(2,1)S(1)}, bf16[4160,128]{1,0:T(8,128)(2,1)S(1)}, u32[]{:S(2)}, u32[]{:S(2)}) collective-permute-start(bf16[4160,128]{1,0:T(8,128)(2,1)S(1)} %pack.13.refs_1_), channel_id=1, source_target_pairs={{0,96},{4,28},{8,104},{12,4},{16,112},{20,12},{24,120},{28,20},{32... | collective-permute-start | bytes 3194888 | tf_op jit(solution)/shard_map/ppermute | solution.py:45
  45.3 2.3 %collective-permute-done.22.refs_0_ = bf16[768,2048]{1,0:T(8,128)(2,1)S(1)} collective-permute-done((bf16[768,2048]{1,0:T(8,128)(2,1)S(1)}, bf16[768,2048]{1,0:T(8,128)(2,1)S(1)}, u32[]{:S(2)}, u32[]{:S(2)}) %collective-permute-start.22) | collective-permute-done | bytes 3145760 | tf_op jit(solution)/shard_map/ppermute | solution.py:49
  47.6 1.8 %shard_map.137 = (bf16[2048,2048]{1,0:T(8,128)(2,1)}, bf16[2048,2048]{1,0:T(8,128)(2,1)}) custom-call(bf16[768,2048]{1,0:T(8,128)(2,1)S(1)} %collective-permute-done.22.refs_0_, bf16[2048,2048]{1,0:T(8,128)(2,1)} %get-tuple-element.36.refs_1_, bf16[2048,2048]{1,0:T(8,128)(2,1)} %get-tuple-element.37.refs_2_), custom_call_target="tpu_custom_call", output_to_operand_aliasing={{0}: (1, {}), {1}: (2, {})} | custom-call | tf_op jit(solution)/shard_map/pallas_call | solution.py:198
  49.4 8.6 %collective-permute-done.17.refs_1_.refs_0_ = bf16[4160,128]{1,0:T(8,128)(2,1)S(1)} collective-permute-done((bf16[4160,128]{1,0:T(8,128)(2,1)S(1)}, bf16[4160,128]{1,0:T(8,128)(2,1)S(1)}, u32[]{:S(2)}, u32[]{:S(2)}) %collective-permute-start.17) | collective-permute-done | bytes 1064992 | tf_op jit(solution)/shard_map/ppermute | solution.py:45
  58.0 2.6 %shard_map.138 = (bf16[512,2048]{1,0:T(8,128)(2,1)S(1)}, bf16[2048,2048]{1,0:T(8,128)(2,1)}, bf16[2048,2048]{1,0:T(8,128)(2,1)}) custom-call(bf16[4160,128]{1,0:T(8,128)(2,1)S(1)} %collective-permute-done.17.refs_1_.refs_0_, bf16[4160,128]{1,0:T(8,128)(2,1)S(1)} %collective-permute-done.20.refs_1_, ...), custom_call_target="tpu_custom_call", output_to_operand_aliasing={{1}: (3, {}), {2}: (4, {})} | custom-call | tf_op jit(solution)/shard_map/pallas_call | solution.py:165
  61.3 2.9 %collective-permute-start.6 = (bf16[2080,128]{1,0:T(8,128)(2,1)S(1)}, bf16[2080,128]{1,0:T(8,128)(2,1)S(1)}, u32[]{:S(2)}, u32[]{:S(2)}) collective-permute-start(bf16[2080,128]{1,0:T(8,128)(2,1)S(1)} %pack.10.refs_2_), channel_id=1, source_target_pairs={{0,96},{4,28},{8,104},{12,4},{16,112},{20,12},{24,120},{28,20},{32... | collective-permute-start | bytes 1597448 | tf_op jit(solution)/shard_map/ppermute | solution.py:45
  66.4 4.7 %collective-permute-done.4.refs_0_ = bf16[2080,128]{1,0:T(8,128)(2,1)S(1)} collective-permute-done((bf16[2080,128]{1,0:T(8,128)(2,1)S(1)}, bf16[2080,128]{1,0:T(8,128)(2,1)S(1)}, u32[]{:S(2)}, u32[]{:S(2)}) %collective-permute-start.4) | collective-permute-done | bytes 532512 | tf_op jit(solution)/shard_map/ppermute | solution.py:45
  74.1 2.7 %collective-permute-start.21 = (bf16[3120,128]{1,0:T(8,128)(2,1)S(1)}, bf16[3120,128]{1,0:T(8,128)(2,1)S(1)}, u32[]{:S(2)}, u32[]{:S(2)}) collective-permute-start(bf16[3120,128]{1,0:T(8,128)(2,1)S(1)} %pack.15), channel_id=1, source_target_pairs={{0,96},{4,28},{8,104},{12,4},{16,112},{20,12},{24,120},{28,20},{32... | collective-permute-start | bytes 2396168 | tf_op jit(solution)/shard_map/ppermute | solution.py:45
  77.8 8.7 %collective-permute-done.18.refs_0_ = bf16[3120,128]{1,0:T(8,128)(2,1)S(1)} collective-permute-done((bf16[3120,128]{1,0:T(8,128)(2,1)S(1)}, bf16[3120,128]{1,0:T(8,128)(2,1)S(1)}, u32[]{:S(2)}, u32[]{:S(2)}) %collective-permute-start.18) | collective-permute-done | bytes 798752 | tf_op jit(solution)/shard_map/ppermute | solution.py:45
  86.5 2.1 %shard_map.142 = (bf16[384,2048]{1,0:T(8,128)(2,1)S(1)}, bf16[2048,2048]{1,0:T(8,128)(2,1)}, bf16[2048,2048]{1,0:T(8,128)(2,1)}) custom-call(bf16[3120,128]{1,0:T(8,128)(2,1)S(1)} %collective-permute-done.18.refs_0_, bf16[3120,128]{1,0:T(8,128)(2,1)S(1)} %collective-permute-done.21.refs_1_, ...), custom_call_target="tpu_custom_call", output_to_operand_aliasing={{1}: (3, {}), {2}: (4, {})} | custom-call | tf_op jit(solution)/shard_map/pallas_call | solution.py:165
  89.8 2.9 %collective-permute-start.7 = (bf16[1040,128]{1,0:T(8,128)(2,1)S(1)}, bf16[1040,128]{1,0:T(8,128)(2,1)S(1)}, u32[]{:S(2)}, u32[]{:S(2)}) collective-permute-start(bf16[1040,128]{1,0:T(8,128)(2,1)S(1)} %pack.12), channel_id=1, source_target_pairs={{0,96},{4,28},{8,104},{12,4},{16,112},{20,12},{24,120},{28,20},{32... | collective-permute-start | bytes 798728 | tf_op jit(solution)/shard_map/ppermute | solution.py:45
  92.7 4.0 %collective-permute-done.5.refs_0_ = bf16[1040,128]{1,0:T(8,128)(2,1)S(1)} collective-permute-done((bf16[1040,128]{1,0:T(8,128)(2,1)S(1)}, bf16[1040,128]{1,0:T(8,128)(2,1)S(1)}, u32[]{:S(2)}, u32[]{:S(2)}) %collective-permute-start.5) | collective-permute-done | bytes 266272 | tf_op jit(solution)/shard_map/ppermute | solution.py:45
  103.0 2.5 %collective-permute-done.28 = f32[16,128]{1,0:T(8,128)S(1)} collective-permute-done((f32[16,128]{1,0:T(8,128)S(1)}, f32[16,128]{1,0:T(8,128)S(1)}, u32[]{:S(2)}, u32[]{:S(2)}) %collective-permute-start.28) | collective-permute-done | bytes 8224 | tf_op jit(solution)/shard_map/ppermute | solution.py:226
  (77 shorter events, 29.3 us)
Async XLA Ops:
  9.6 14.0 %collective-permute-start = (bf16[2080,128]{1,0:T(8,128)(2,1)S(1)}, bf16[2080,128]{1,0:T(8,128)(2,1)S(1)}, u32[]{:S(2)}, u32[]{:S(2)}) collective-permute-start(bf16[2080,128]{1,0:T(8,128)(2,1)S(1)} %get-tuple-element.33.refs_0_), channel_id=1, source_target_pairs={{0,8},{4,36},{8,16},{12,44},{16,24},{20,52},{24,0},{28,60},{32,40}... | collective-permute-start | bytes 1597448 | tf_op jit(solution)/shard_map/ppermute | solution.py:41
  12.2 14.1 %collective-permute-start.2 = (bf16[2080,128]{1,0:T(8,128)(2,1)S(1)}, bf16[2080,128]{1,0:T(8,128)(2,1)S(1)}, u32[]{:S(2)}, u32[]{:S(2)}) collective-permute-start(bf16[2080,128]{1,0:T(8,128)(2,1)S(1)} %get-tuple-element.33.refs_0_), channel_id=1, source_target_pairs={{0,24},{4,100},{8,0},{12,108},{16,8},{20,116},{24,16},{28,124},{32... | collective-permute-start | bytes 1597448 | tf_op jit(solution)/shard_map/ppermute | solution.py:41
  15.2 5.7 %collective-permute-start.10 = (f32[48,128]{1,0:T(8,128)S(1)}, f32[48,128]{1,0:T(8,128)S(1)}, u32[]{:S(2)}, u32[]{:S(2)}) collective-permute-start(f32[48,128]{1,0:T(8,128)S(1)} %constant_dynamic-update-slice_fusion), channel_id=1, source_target_pairs={{0,64},{4,20},{8,72},{12,28},{16,80},{20,4},{24,88},{28,12},{32,96... | collective-permute-start | bytes 73736 | tf_op jit(solution)/shard_map/ppermute | solution.py:45
  18.6 5.0 %collective-permute-start.9 = (f32[48,128]{1,0:T(8,128)S(1)}, f32[48,128]{1,0:T(8,128)S(1)}, u32[]{:S(2)}, u32[]{:S(2)}) collective-permute-start(f32[48,128]{1,0:T(8,128)S(1)} %constant_dynamic-update-slice_fusion), channel_id=1, source_target_pairs={{0,96},{4,28},{8,104},{12,4},{16,112},{20,12},{24,120},{28,20},{32... | collective-permute-start | bytes 73736 | tf_op jit(solution)/shard_map/ppermute | solution.py:45
  20.8 15.4 %collective-permute-start.16 = (bf16[2080,128]{1,0:T(8,128)(2,1)S(1)}, bf16[2080,128]{1,0:T(8,128)(2,1)S(1)}, u32[]{:S(2)}, u32[]{:S(2)}) collective-permute-start(bf16[2080,128]{1,0:T(8,128)(2,1)S(1)} %get-tuple-element.33.refs_0_), channel_id=1, source_target_pairs={{0,32},{4,12},{8,40},{12,20},{16,48},{20,28},{24,56},{28,4},{32,64... | collective-permute-start | bytes 1597448 | tf_op jit(solution)/shard_map/ppermute | solution.py:45
  22.0 14.2 %collective-permute-start.19 = (bf16[2080,128]{1,0:T(8,128)(2,1)S(1)}, bf16[2080,128]{1,0:T(8,128)(2,1)S(1)}, u32[]{:S(2)}, u32[]{:S(2)}) collective-permute-start(bf16[2080,128]{1,0:T(8,128)(2,1)S(1)} %get-tuple-element.33.refs_0_), channel_id=1, source_target_pairs={{0,96},{4,28},{8,104},{12,4},{16,112},{20,12},{24,120},{28,20},{32... | collective-permute-start | bytes 1597448 | tf_op jit(solution)/shard_map/ppermute | solution.py:45
  23.5 4.5 %collective-permute-start.11 = (f32[48,128]{1,0:T(8,128)S(1)}, f32[48,128]{1,0:T(8,128)S(1)}, u32[]{:S(2)}, u32[]{:S(2)}) collective-permute-start(f32[48,128]{1,0:T(8,128)S(1)} %add_add_fusion.1), channel_id=1, source_target_pairs={{0,8},{4,36},{8,16},{12,44},{16,24},{20,52},{24,0},{28,60},{32,40}... | collective-permute-start | bytes 73736 | tf_op jit(solution)/shard_map/ppermute | solution.py:41
  23.6 4.4 %collective-permute-start.12 = (f32[48,128]{1,0:T(8,128)S(1)}, f32[48,128]{1,0:T(8,128)S(1)}, u32[]{:S(2)}, u32[]{:S(2)}) collective-permute-start(f32[48,128]{1,0:T(8,128)S(1)} %add_add_fusion.1), channel_id=1, source_target_pairs={{0,24},{4,100},{8,0},{12,108},{16,8},{20,116},{24,16},{28,124},{32... | collective-permute-start | bytes 73736 | tf_op jit(solution)/shard_map/ppermute | solution.py:41
  26.3 4.5 %collective-permute-start.13 = (f32[48,128]{1,0:T(8,128)S(1)}, f32[48,128]{1,0:T(8,128)S(1)}, u32[]{:S(2)}, u32[]{:S(2)}) collective-permute-start(f32[48,128]{1,0:T(8,128)S(1)} %add_add_fusion.1), channel_id=1, source_target_pairs={{0,16},{4,68},{8,24},{12,76},{16,0},{20,84},{24,8},{28,92},{32,48}... | collective-permute-start | bytes 73736 | tf_op jit(solution)/shard_map/ppermute | solution.py:41
  28.1 7.8 %collective-permute-start.1 = (bf16[1040,128]{1,0:T(8,128)(2,1)S(1)}, bf16[1040,128]{1,0:T(8,128)(2,1)S(1)}, u32[]{:S(2)}, u32[]{:S(2)}) collective-permute-start(bf16[1040,128]{1,0:T(8,128)(2,1)S(1)} %pack.8), channel_id=1, source_target_pairs={{0,8},{4,36},{8,16},{12,44},{16,24},{20,52},{24,0},{28,60},{32,40}... | collective-permute-start | bytes 798728 | tf_op jit(solution)/shard_map/ppermute | solution.py:41
  28.1 8.2 %collective-permute-start.3 = (bf16[1040,128]{1,0:T(8,128)(2,1)S(1)}, bf16[1040,128]{1,0:T(8,128)(2,1)S(1)}, u32[]{:S(2)}, u32[]{:S(2)}) collective-permute-start(bf16[1040,128]{1,0:T(8,128)(2,1)S(1)} %pack.9), channel_id=1, source_target_pairs={{0,24},{4,100},{8,0},{12,108},{16,8},{20,116},{24,16},{28,124},{32... | collective-permute-start | bytes 798728 | tf_op jit(solution)/shard_map/ppermute | solution.py:41
  30.8 4.5 %collective-permute-start.14 = (f32[48,128]{1,0:T(8,128)S(1)}, f32[48,128]{1,0:T(8,128)S(1)}, u32[]{:S(2)}, u32[]{:S(2)}) collective-permute-start(f32[48,128]{1,0:T(8,128)S(1)} %add_add_fusion), channel_id=1, source_target_pairs={{0,4},{4,0},{1,5},{5,1},{2,6},{6,2},{3,7},{7,3},{8,12},{12,8},{9,1... | collective-permute-start | bytes 73736 | tf_op jit(solution)/shard_map/ppermute | solution.py:49
  39.8 7.8 %collective-permute-start.22 = (bf16[768,2048]{1,0:T(8,128)(2,1)S(1)}, bf16[768,2048]{1,0:T(8,128)(2,1)S(1)}, u32[]{:S(2)}, u32[]{:S(2)}) collective-permute-start(bf16[768,2048]{1,0:T(8,128)(2,1)S(1)} %get-tuple-element.35), channel_id=1, source_target_pairs={{0,4},{4,0},{1,5},{5,1},{2,6},{6,2},{3,7},{7,3},{8,12},{12,8},{9,1... | collective-permute-start | bytes 9437192 | tf_op jit(solution)/shard_map/ppermute | solution.py:49
  42.3 15.6 %collective-permute-start.17 = (bf16[4160,128]{1,0:T(8,128)(2,1)S(1)}, bf16[4160,128]{1,0:T(8,128)(2,1)S(1)}, u32[]{:S(2)}, u32[]{:S(2)}) collective-permute-start(bf16[4160,128]{1,0:T(8,128)(2,1)S(1)} %pack.13.refs_1_), channel_id=1, source_target_pairs={{0,32},{4,12},{8,40},{12,20},{16,48},{20,28},{24,56},{28,4},{32,64... | collective-permute-start | bytes 3194888 | tf_op jit(solution)/shard_map/ppermute | solution.py:45
  42.4 15.5 %collective-permute-start.20 = (bf16[4160,128]{1,0:T(8,128)(2,1)S(1)}, bf16[4160,128]{1,0:T(8,128)(2,1)S(1)}, u32[]{:S(2)}, u32[]{:S(2)}) collective-permute-start(bf16[4160,128]{1,0:T(8,128)(2,1)S(1)} %pack.13.refs_1_), channel_id=1, source_target_pairs={{0,96},{4,28},{8,104},{12,4},{16,112},{20,12},{24,120},{28,20},{32... | collective-permute-start | bytes 3194888 | tf_op jit(solution)/shard_map/ppermute | solution.py:45
  60.5 4.5 %collective-permute-start.23 = (bf16[512,2048]{1,0:T(8,128)(2,1)S(1)}, bf16[512,2048]{1,0:T(8,128)(2,1)S(1)}, u32[]{:S(2)}, u32[]{:S(2)}) collective-permute-start(bf16[512,2048]{1,0:T(8,128)(2,1)S(1)} %get-tuple-element.40), channel_id=1, source_target_pairs={{0,4},{4,0},{1,5},{5,1},{2,6},{6,2},{3,7},{7,3},{8,12},{12,8},{9,1... | collective-permute-start | bytes 6291464 | tf_op jit(solution)/shard_map/ppermute | solution.py:49
  61.3 9.9 %collective-permute-start.4 = (bf16[2080,128]{1,0:T(8,128)(2,1)S(1)}, bf16[2080,128]{1,0:T(8,128)(2,1)S(1)}, u32[]{:S(2)}, u32[]{:S(2)}) collective-permute-start(bf16[2080,128]{1,0:T(8,128)(2,1)S(1)} %pack.10.refs_2_), channel_id=1, source_target_pairs={{0,32},{4,12},{8,40},{12,20},{16,48},{20,28},{24,56},{28,4},{32,64... | collective-permute-start | bytes 1597448 | tf_op jit(solution)/shard_map/ppermute | solution.py:45
  61.3 9.8 %collective-permute-start.6 = (bf16[2080,128]{1,0:T(8,128)(2,1)S(1)}, bf16[2080,128]{1,0:T(8,128)(2,1)S(1)}, u32[]{:S(2)}, u32[]{:S(2)}) collective-permute-start(bf16[2080,128]{1,0:T(8,128)(2,1)S(1)} %pack.10.refs_2_), channel_id=1, source_target_pairs={{0,96},{4,28},{8,104},{12,4},{16,112},{20,12},{24,120},{28,20},{32... | collective-permute-start | bytes 1597448 | tf_op jit(solution)/shard_map/ppermute | solution.py:45
  73.6 12.8 %collective-permute-start.18 = (bf16[3120,128]{1,0:T(8,128)(2,1)S(1)}, bf16[3120,128]{1,0:T(8,128)(2,1)S(1)}, u32[]{:S(2)}, u32[]{:S(2)}) collective-permute-start(bf16[3120,128]{1,0:T(8,128)(2,1)S(1)} %pack.14), channel_id=1, source_target_pairs={{0,32},{4,12},{8,40},{12,20},{16,48},{20,28},{24,56},{28,4},{32,64... | collective-permute-start | bytes 2396168 | tf_op jit(solution)/shard_map/ppermute | solution.py:45
  74.1 12.4 %collective-permute-start.21 = (bf16[3120,128]{1,0:T(8,128)(2,1)S(1)}, bf16[3120,128]{1,0:T(8,128)(2,1)S(1)}, u32[]{:S(2)}, u32[]{:S(2)}) collective-permute-start(bf16[3120,128]{1,0:T(8,128)(2,1)S(1)} %pack.15), channel_id=1, source_target_pairs={{0,96},{4,28},{8,104},{12,4},{16,112},{20,12},{24,120},{28,20},{32... | collective-permute-start | bytes 2396168 | tf_op jit(solution)/shard_map/ppermute | solution.py:45
  88.6 17.5 %collective-permute-start.25 = (bf16[384,2048]{1,0:T(8,128)(2,1)S(1)}, bf16[384,2048]{1,0:T(8,128)(2,1)S(1)}, u32[]{:S(2)}, u32[]{:S(2)}) collective-permute-start(bf16[384,2048]{1,0:T(8,128)(2,1)S(1)} %get-tuple-element.50), channel_id=1, source_target_pairs={{0,4},{4,0},{1,5},{5,1},{2,6},{6,2},{3,7},{7,3},{8,12},{12,8},{9,1... | collective-permute-start | bytes 4718600 | tf_op jit(solution)/shard_map/ppermute | solution.py:49
  89.6 7.1 %collective-permute-start.5 = (bf16[1040,128]{1,0:T(8,128)(2,1)S(1)}, bf16[1040,128]{1,0:T(8,128)(2,1)S(1)}, u32[]{:S(2)}, u32[]{:S(2)}) collective-permute-start(bf16[1040,128]{1,0:T(8,128)(2,1)S(1)} %pack.11), channel_id=1, source_target_pairs={{0,32},{4,12},{8,40},{12,20},{16,48},{20,28},{24,56},{28,4},{32,64... | collective-permute-start | bytes 798728 | tf_op jit(solution)/shard_map/ppermute | solution.py:45
  89.8 6.9 %collective-permute-start.7 = (bf16[1040,128]{1,0:T(8,128)(2,1)S(1)}, bf16[1040,128]{1,0:T(8,128)(2,1)S(1)}, u32[]{:S(2)}, u32[]{:S(2)}) collective-permute-start(bf16[1040,128]{1,0:T(8,128)(2,1)S(1)} %pack.12), channel_id=1, source_target_pairs={{0,96},{4,28},{8,104},{12,4},{16,112},{20,12},{24,120},{28,20},{32... | collective-permute-start | bytes 798728 | tf_op jit(solution)/shard_map/ppermute | solution.py:45
  97.2 10.1 %collective-permute-start.15 = (bf16[128,2048]{1,0:T(8,128)(2,1)S(1)}, bf16[128,2048]{1,0:T(8,128)(2,1)S(1)}, u32[]{:S(2)}, u32[]{:S(2)}) collective-permute-start(bf16[128,2048]{1,0:T(8,128)(2,1)S(1)} %shard_map.135.refs_0_), channel_id=1, source_target_pairs={{0,4},{4,0},{1,5},{5,1},{2,6},{6,2},{3,7},{7,3},{8,12},{12,8},{9,1... | collective-permute-start | bytes 1572872 | tf_op jit(solution)/shard_map/ppermute | solution.py:49
  (11 other events, 25.3 us)
